TPU v7x, 32 devices: a whole 2x2x4 slice. The times are simulated.
32 devices in a mesh: blk: 16 (over z, y, core), head: 2 (over x).
Axes of the slice: x: 2, y: 2, z: 4, core: 2. Of those that a mesh axis runs over, the one named last changes fastest.
Arguments:
- queries: bfloat16 [4096, 1024], P('blk', 'head'), may hold values from -216 to 216
- keys: bfloat16 [4096, 1024], P('blk', 'head'), may hold values from -6 to 6
- values: bfloat16 [4096, 1024], P('blk', 'head'), may hold values from -6 to 6
- group_table: int32 [16, 2], P('blk'), may hold values from 0 to 31, as said below
- doc_ids: int32 [4096], replicated, may hold values from 0 to 15, never falling along the last dimension, each value on 1 to 2048 neighbouring positions
Outputs:
- attended: bfloat16 [4096, 1024], P('blk', 'head')
Inputs may be any that keep to these rules, and one draw needn't show every extreme that they name: group_table[d, 1] = 31 - group_table[d, 0]; the first column holds each of 0 to 15 once. `doc_ids`: document numbers never fall along positions; a document holds at most 2048 positions.
All inputs are finite; a program needn't handle non-finite values.
Results may differ from a plain program's by a relative error of at most 0.0049.
Values may be sent and summed in bfloat16 or wider, within the bound.
A program may use at most 192 MiB of HBM per device.

v0:
```python
import math
import jax
import jax.numpy as jnp
from jax import lax
from jax.sharding import PartitionSpec as P

HEAD_DIM = 128


def shards(queries, keys, values, group_table, doc_ids):
    tok_rows = queries.shape[0]
    group_rows = tok_rows // 2
    head_count = queries.shape[1] // HEAD_DIM
    score_scale = 1.0 / math.sqrt(HEAD_DIM)
    whole_table = lax.all_gather(group_table, "blk", axis=0, tiled=True)
    group_docs = doc_ids.reshape(doc_ids.shape[0] // group_rows, group_rows)
    within = jnp.arange(group_rows, dtype=jnp.int32)
    stored_groups = whole_table.reshape(-1)
    all_key_pos = (stored_groups[:, None] * group_rows + within[None, :]).reshape(-1)
    all_key_doc = group_docs[stored_groups].reshape(-1)
    local_groups = group_table.reshape(-1)
    query_pos = (local_groups[:, None] * group_rows + within[None, :]).reshape(-1)
    query_doc = group_docs[local_groups].reshape(-1)
    query_heads = queries.reshape(tok_rows, head_count, HEAD_DIM)

    def attend_shard(running_state, key_piece, value_piece, offset):
        piece_rows = key_piece.shape[0]
        key_pos = lax.dynamic_slice_in_dim(all_key_pos, offset, piece_rows, 0)
        key_doc = lax.dynamic_slice_in_dim(all_key_doc, offset, piece_rows, 0)
        visible = (query_doc[:, None] == key_doc[None, :]) & (
            key_pos[None, :] <= query_pos[:, None]
        )
        summed, running_max, weight_sum = running_state
        key_heads = key_piece.reshape(piece_rows, head_count, HEAD_DIM)
        value_heads = value_piece.reshape(piece_rows, head_count, HEAD_DIM)
        scores = (
            jnp.einsum("qhd,khd->hqk", query_heads, key_heads, preferred_element_type=jnp.float32)
            * score_scale
        )
        scores = jnp.where(visible[None], scores, -1e30)
        new_max = jnp.maximum(running_max, jnp.max(scores, axis=-1))
        weights = jnp.where(visible[None], jnp.exp(scores - new_max[..., None]), 0.0)
        factor = jnp.exp(running_max - new_max)
        weight_sum = weight_sum * factor + jnp.sum(weights, axis=-1)
        summed = summed * jnp.transpose(factor)[..., None] + jnp.einsum(
            "hqk,khd->qhd",
            weights.astype(jnp.bfloat16),
            value_heads,
            preferred_element_type=jnp.float32,
        )
        return (summed, new_max, weight_sum)

    initial = (
        jnp.zeros((tok_rows, head_count, HEAD_DIM), jnp.float32),
        jnp.full((head_count, tok_rows), -1e30, jnp.float32),
        jnp.zeros((head_count, tok_rows), jnp.float32),
    )
    key_piece = lax.all_gather(keys, "blk", axis=0, tiled=True)
    value_piece = lax.all_gather(values, "blk", axis=0, tiled=True)
    shard_count = key_piece.shape[0] // tok_rows
    key_shards = key_piece.reshape(shard_count, tok_rows, key_piece.shape[1])
    value_shards = value_piece.reshape(shard_count, tok_rows, value_piece.shape[1])
    shard_ids = jnp.arange(shard_count, dtype=jnp.int32)

    def step(state_now, item):
        key_one, value_one, shard_index = item
        start = shard_index * tok_rows
        return (attend_shard(state_now, key_one, value_one, start), None)

    final_state, unused = lax.scan(step, initial, (key_shards, value_shards, shard_ids))
    summed, running_max, weight_sum = final_state
    output = summed / jnp.transpose(weight_sum)[..., None]
    return output.reshape(tok_rows, head_count * HEAD_DIM).astype(jnp.bfloat16)


def solution(mesh):
    in_specs = (P("blk", "head"), P("blk", "head"), P("blk", "head"), P("blk", None), P())
    out_specs = P("blk", "head")
    return jax.shard_map(shards, mesh=mesh, in_specs=in_specs, out_specs=out_specs, check_vma=False)
```

profile of v0, /device:TPU:0, one launch (start us, length us, event | category | flops | bytes accessed | tf_op | source)
XLA Modules:
  0.0 186.2 jit_solution(14628548293793121357)
XLA Ops:
  6.5 0.7 all-gather.4.cloned.1.call-update
  7.3 0.7 all-gather.6.cloned.1.call-update
  8.0 23.3 %all-gather = s32[16,1,2]{2,1,0:T(1,128)S(1)} all-gather(s32[1,1,2]{2,1,0:T(1,128)} %bitcast.68), channel_id=1, replica_groups=mesh['blk'=16,'head'=2] {'blk'}, dimensions={0}, use_global_device_ids=true | all-gather | bytes 136 | tf_op jit(solution)/shard_map/all_gather | solution.py:15
  31.4 0.5 broadcast.150
  31.9 0.7 multiply_reduce_fusion
  32.8 0.6 gather_fusion.1
  33.3 0.7 fusion.14
  34.0 0.6 gather_fusion
  34.6 1.1 copy.23
  35.8 0.7 multiply_bitcast_fusion
  36.6 26.1 %all-gather.4.cloned.1.call-done = bf16[4096,512]{1,0:T(8,128)(2,1)} async-done(((bf16[256,512]{1,0:T(8,128)(2,1)}), bf16[4096,512]{1,0:T(8,128)(2,1)}) %all-gather.4.cloned.1.call-update) | async-done | bytes 4194320 | tf_op jit(solution)/shard_map/all_gather | solution.py:58
  62.7 51.1 %all-gather.6.cloned.1.call-done = bf16[4096,512]{1,0:T(8,128)(2,1)} async-done(((bf16[256,512]{1,0:T(8,128)(2,1)}), bf16[4096,512]{1,0:T(8,128)(2,1)}) %all-gather.6.cloned.1.call-update) | async-done | bytes 4194320 | tf_op jit(solution)/shard_map/all_gather | solution.py:59
  113.8 64.7 %while.15 = (s32[]{:T(128)}, f32[256,4,128]{0,2,1:T(8,128)S(1)}, f32[4,256]{1,0:T(4,128)S(1)}, f32[4,256]{1,0:T(4,128)S(1)}, s32[2,128]{1,0:T(2,128)S(1)}, /*ind...) while((s32[]{:T(128)}, f32[256,4,128]{0,2,1:T(8,128)S(1)}, ...), condition=%wide.region_3.4_spmd.clone, body=%wide.region_0.3_spmd.clone.sunk | while | flops 137173248 | bytes 7415023 | solution.py:70
  113.8 0.6 dynamic_slice.29
  115.4 1.1 constant_dynamic-slice_fusion.3
  117.4 0.4 fusion.35
  117.8 0.6 dynamic_slice.29
  119.4 1.1 constant_dynamic-slice_fusion.3
  121.9 0.6 dynamic_slice.29
  123.5 1.1 constant_dynamic-slice_fusion.3
  125.4 0.4 fusion.35
  125.9 0.6 dynamic_slice.29
  127.5 1.1 constant_dynamic-slice_fusion.3
  129.9 0.6 dynamic_slice.29
  131.5 1.1 constant_dynamic-slice_fusion.3
  134.0 0.6 dynamic_slice.29
  135.6 1.1 constant_dynamic-slice_fusion.3
  138.0 0.6 dynamic_slice.29
  139.6 1.1 constant_dynamic-slice_fusion.3
  142.1 0.6 dynamic_slice.29
  143.7 1.1 constant_dynamic-slice_fusion.3
  146.1 0.6 dynamic_slice.29
  147.7 1.1 constant_dynamic-slice_fusion.3
  150.2 0.6 dynamic_slice.29
  151.8 1.1 constant_dynamic-slice_fusion.3
  154.2 0.6 dynamic_slice.29
  155.8 1.1 constant_dynamic-slice_fusion.3
  158.2 0.6 dynamic_slice.29
  159.8 1.1 constant_dynamic-slice_fusion.3
  162.3 0.6 dynamic_slice.29
  163.9 1.1 constant_dynamic-slice_fusion.3
  166.3 0.6 dynamic_slice.29
  167.9 1.1 constant_dynamic-slice_fusion.3
  170.4 0.6 dynamic_slice.29
  172.0 1.1 constant_dynamic-slice_fusion.3
  174.4 0.6 dynamic_slice.29
  176.0 1.1 constant_dynamic-slice_fusion.3
  178.5 0.8 copy.30
  (206 shorter events, 26.2 us)
Async XLA Ops:
  6.5 26.2 %copy-start = (s32[4096]{0:T(1024)S(1)}, s32[4096]{0:T(1024)}, u32[]{:S(2)}) copy-start(s32[4096]{0:T(1024)} %param.11) | copy-start | bytes 49156
  6.5 56.1 %all-gather.4.cloned.1.call-start = ((), (), s32[]{:S(2)}) async-start(), calls=%async_computation | async-start | bytes 4456448 | tf_op jit(solution)/shard_map/all_gather | solution.py:58
  7.3 106.5 %all-gather.6.cloned.1.call-start = ((), (), s32[]{:S(2)}) async-start(), calls=%async_computation.1 | async-start | bytes 4456448 | tf_op jit(solution)/shard_map/all_gather | solution.py:59
Sparse Core Ops, SparseCore 0:
  9.5 53.1 all-gather.3
  64.8 48.8 all-gather.5
where the time goes:
time: 187 us; the launch traced here: 186 us
  waiting for transfers between devices  78.6 us (42%)
  local copies, waits for them, and re-layouts  37.4 us (20%)
  blocking collectives  23.3 us (12%)
  between operations  13.5 us (7%)
  matrix products  12.7 us (7%)
  loops' own time  11.4 us (6%)
  other arithmetic  9.23 us (5%)
    all_gather x1, waiting for transfers between devices, shards(): value_piece = lax.all_gather(values, 'blk', axis=0, tiled=True)  51.1 us
    dynamic_slice x64, local copies, waits for them, and re-layouts, shards(): lax.scan(step, initial, (key_shards, value_shards, shard_ids))  31 us
    all_gather x1, waiting for transfers between devices, shards(): key_piece = lax.all_gather(keys, 'blk', axis=0, tiled=True)  26.1 us
    all_gather x1, blocking collectives, shards(): whole_table = lax.all_gather(group_table, 'blk', axis=0, tiled=True)  23.3 us
    another operation x1, loops' own time, shards(): lax.scan(step, initial, (key_shards, value_shards, shard_ids))  11.4 us
    dot_general x16, matrix products, attend_shard(): jnp.einsum('hqk,khd->qhd', weights.astype(jnp.bfloat16), value_heads, pre...  6.68 us
    dot_general x16, matrix products, attend_shard(): jnp.einsum('qhd,khd->hqk', query_heads, key_heads, preferred_element_type...  6.02 us
  transfers between devices with their start and end apart: 2, of which 2 were waited for; matrix products, arithmetic and copies ran while one was open for 3% of the time, Pallas kernels for 0%

commit v1 on v0

--- a/solution.py
+++ b/solution.py
@@ -55,8 +55,11 @@
         jnp.full((head_count, tok_rows), -1e30, jnp.float32),
         jnp.zeros((head_count, tok_rows), jnp.float32),
     )
-    key_piece = lax.all_gather(keys, "blk", axis=0, tiled=True)
-    value_piece = lax.all_gather(values, "blk", axis=0, tiled=True)
+    key_piece, value_piece = jnp.split(
+        lax.all_gather(jnp.concatenate([keys, values], axis=1), "blk", axis=0, tiled=True),
+        [keys.shape[1]],
+        axis=1,
+    )
     shard_count = key_piece.shape[0] // tok_rows
     key_shards = key_piece.reshape(shard_count, tok_rows, key_piece.shape[1])
     value_shards = value_piece.reshape(shard_count, tok_rows, value_piece.shape[1])

time: 187 us -> 167 us (0.89)
  waiting for transfers between devices: 78.6 us -> 49.2 us
  local copies, waits for them, and re-layouts: 37.4 us -> 44.2 us
  other arithmetic: 9.23 us -> 11.2 us
    all_gather x2 -> x1, waiting for transfers between devices: 77.2 us -> 49.2 us  [shards(): lax.all_gather(jnp.concatenate([keys, values], axis=1), 'blk', axis=0, ti...]
    split x0 -> x1, local copies, waits for them, and re-layouts: none -> 5.72 us  [shards(): jnp.split(lax.all_gather(jnp.concatenate([keys, values], axis=1), 'blk',...]
    concatenate x0 -> x1, other arithmetic: none -> 1.94 us  [shards(): jnp.concatenate([keys, values], axis=1)]
  transfers between devices with their start and end apart: 2 -> 1, of which waited for: 2 -> 1; matrix products, arithmetic and copies ran while one was open for 3% -> 3% of each run, Pallas kernels for 0% -> 0%
where the time goes in v1:
time: 167 us
  waiting for transfers between devices  49.2 us (29%)
  local copies, waits for them, and re-layouts  44.2 us (26%)
  blocking collectives  23.6 us (14%)
  between operations  13.5 us (8%)
  matrix products  12.5 us (7%)
  loops' own time  12.4 us (7%)
  other arithmetic  11.2 us (7%)
    all_gather x1, waiting for transfers between devices, shards(): lax.all_gather(jnp.concatenate([keys, values], axis=1), 'blk', axis=0, ti...  49.2 us
    dynamic_slice x64, local copies, waits for them, and re-layouts, shards(): lax.scan(step, initial, (key_shards, value_shards, shard_ids))  32.1 us
    all_gather x1, blocking collectives, shards(): whole_table = lax.all_gather(group_table, 'blk', axis=0, tiled=True)  23.6 us
    another operation x1, loops' own time, shards(): lax.scan(step, initial, (key_shards, value_shards, shard_ids))  12.4 us
    dot_general x16, matrix products, attend_shard(): jnp.einsum('hqk,khd->qhd', weights.astype(jnp.bfloat16), value_heads, pre...  6.57 us
    dot_general x16, matrix products, attend_shard(): jnp.einsum('qhd,khd->hqk', query_heads, key_heads, preferred_element_type...  5.94 us
    split x1, local copies, waits for them, and re-layouts, shards(): jnp.split(lax.all_gather(jnp.concatenate([keys, values], axis=1), 'blk',...  5.72 us
  transfers between devices with their start and end apart: 1, of which 1 were waited for; matrix products, arithmetic and copies ran while one was open for 3% of the time, Pallas kernels for 0%

profile of v1, /device:TPU:0, one launch (start us, length us, event | category | flops | bytes accessed | tf_op | source)
XLA Modules:
  0.0 166.6 jit_solution(4867497972745188091)
XLA Ops:
  6.5 1.9 %pad_maximum_fusion = bf16[256,1024]{1,0:T(8,128)(2,1)} fusion(bf16[256,512]{1,0:T(8,128)(2,1)} %param.9, bf16[256,512]{1,0:T(8,128)(2,1)} %param.8), kind=kLoop, calls=%fused_computation.25 | loop fusion | flops 1048576 | bytes 1048576 | tf_op jit(solution)/shard_map/concatenate | solution.py:59
  8.5 23.6 %all-gather = s32[16,1,2]{2,1,0:T(1,128)S(1)} all-gather(s32[1,1,2]{2,1,0:T(1,128)} %bitcast.68), channel_id=1, replica_groups=mesh['blk'=16,'head'=2] {'blk'}, dimensions={0}, use_global_device_ids=true | all-gather | bytes 136 | tf_op jit(solution)/shard_map/all_gather | solution.py:15
  32.1 0.5 broadcast.150
  32.7 0.7 multiply_reduce_fusion
  33.6 0.6 gather_fusion.1
  34.1 0.7 fusion.14
  34.8 0.6 gather_fusion
  35.4 1.1 copy.17
  36.6 0.7 multiply_bitcast_fusion
  37.4 49.2 %all-gather.3.cloned.1.call-done = bf16[4096,1024]{1,0:T(8,128)(2,1)} async-done(((bf16[256,1024]{1,0:T(8,128)(2,1)}), bf16[4096,1024]{1,0:T(8,128)(2,1)}) %all-gather.3.cloned.1.call-update) | async-done | bytes 8388624 | tf_op jit(solution)/shard_map/all_gather | solution.py:59
  86.6 5.7 %fusion.17 = (bf16[4096,512]{1,0:T(8,128)(2,1)}, bf16[4096,512]{1,0:T(8,128)(2,1)}) fusion(bf16[4096,1024]{1,0:T(8,128)(2,1)} %all-gather.3.cloned.1.call-done), kind=kLoop, calls=%fused_computation.37 | loop fusion | bytes 16777216 | tf_op jit(solution)/shard_map/split | solution.py:58
  92.3 66.5 %while.15 = (s32[]{:T(128)}, f32[256,4,128]{0,2,1:T(8,128)S(1)}, f32[4,256]{1,0:T(4,128)S(1)}, f32[4,256]{1,0:T(4,128)S(1)}, s32[2,128]{1,0:T(2,128)S(1)}, /*ind...) while((s32[]{:T(128)}, f32[256,4,128]{0,2,1:T(8,128)S(1)}, ...), condition=%wide.region_3.4_spmd.clone, body=%wide.region_0.3_spmd.clone.sunk | while | flops 137173248 | bytes 7415023 | solution.py:73
  92.3 0.7 dynamic_slice.29
  94.0 1.1 constant_dynamic-slice_fusion.3
  96.0 0.4 fusion.36
  96.4 0.7 dynamic_slice.29
  98.2 1.1 constant_dynamic-slice_fusion.3
  100.2 0.4 fusion.36
  100.6 0.7 dynamic_slice.29
  102.3 1.1 constant_dynamic-slice_fusion.3
  104.3 0.4 fusion.36
  104.8 0.7 dynamic_slice.29
  106.5 1.1 constant_dynamic-slice_fusion.3
  108.9 0.7 dynamic_slice.29
  110.7 1.1 constant_dynamic-slice_fusion.3
  113.1 0.7 dynamic_slice.29
  114.8 1.1 constant_dynamic-slice_fusion.3
  117.2 0.7 dynamic_slice.29
  119.0 1.1 constant_dynamic-slice_fusion.3
  121.4 0.7 dynamic_slice.29
  123.1 1.1 constant_dynamic-slice_fusion.3
  125.6 0.7 dynamic_slice.29
  127.3 1.1 constant_dynamic-slice_fusion.3
  129.7 0.7 dynamic_slice.29
  131.5 1.1 constant_dynamic-slice_fusion.3
  133.9 0.7 dynamic_slice.29
  135.6 1.1 constant_dynamic-slice_fusion.3
  138.0 0.7 dynamic_slice.29
  139.8 1.1 constant_dynamic-slice_fusion.3
  142.2 0.7 dynamic_slice.29
  143.9 1.1 constant_dynamic-slice_fusion.3
  146.4 0.7 dynamic_slice.29
  148.1 1.1 constant_dynamic-slice_fusion.3
  150.5 0.7 dynamic_slice.29
  152.3 1.1 constant_dynamic-slice_fusion.3
  154.7 0.7 dynamic_slice.29
  156.4 1.1 constant_dynamic-slice_fusion.3
  158.9 0.8 copy.24
  (205 shorter events, 25.6 us)
Async XLA Ops:
  6.5 27.0 %copy-start = (s32[4096]{0:T(1024)S(1)}, s32[4096]{0:T(1024)}, u32[]{:S(2)}) copy-start(s32[4096]{0:T(1024)} %param.11) | copy-start | bytes 49156
  6.5 80.0 %all-gather.3.cloned.1.call-start = ((), (), s32[]{:S(2)}) async-start(), calls=%async_computation | async-start | bytes 8912896 | tf_op jit(solution)/shard_map/all_gather | solution.py:59
Sparse Core Ops, SparseCore 0:
  9.5 77.0 all-gather.2
